TPU v7x, 256 devices: a whole 4x4x8 slice. The times are simulated.
256 devices in a mesh: tower: 2 (over x_lo), blk: 128 (over z, y, x_hi, core).
Axes of the slice: x: 4 (x_hi: 2, x_lo: 2; x = x_hi * 2 + x_lo), y: 4, z: 8, core: 2. Of those that a mesh axis runs over, the one named last changes fastest.
Arguments:
- pooled: bfloat16 [2, 16384, 1152], P('tower', 'blk'), may hold values from -6 to 6
- final_gain: float32 [2, 1152], P('tower'), may hold values from 0.5 to 1.5
- head_weight: bfloat16 [2, 1152, 1152], P('tower'), may hold values from -0.1875 to 0.1875
- pair_ids: int32 [16384], replicated, may hold values from 0 to 16383
- log_scale: float32 [1], replicated, may hold values from 4.2 to 4.7
- bias: float32 [1], replicated, may hold values from -4 to -1
Outputs:
- emb_grad: float32 [2, 16384, 1152], P('tower', 'blk')
Inputs may be any that keep to these rules, and one draw needn't show every extreme that they name: `pair_ids`: examples with equal ids form positive pairs; every example is a positive pair with its own image and text.
All inputs are finite; a program needn't handle non-finite values.
Results may differ from a plain program's by a relative error of at most 0.0043.
Values may be sent and summed in bfloat16 or wider, within the bound.
No kernel may reach another device: no remote copies, remote signals or barrier semaphores. Data moves between devices by JAX's collectives and lax.ppermute only.
A program may use at most 192 MiB of HBM per device.

v0:
```python
import jax
import jax.numpy as jnp
from jax import lax
from jax.sharding import PartitionSpec as P


def partner(value, axis, stride):
    mask = 2**stride
    pairs = [(source, source ^ mask) for source in range(lax.axis_size(axis))]
    return lax.ppermute(value, axis, pairs)


def embed_rows(feats, gain, weight):
    values = feats.astype(jnp.float32)
    center = values - jnp.mean(values, axis=-1, keepdims=True)
    spread = jnp.mean(center * center, axis=-1, keepdims=True)
    normed = (center * lax.rsqrt(spread + 1e-06) * gain).astype(jnp.bfloat16)
    head = jnp.dot(normed, weight, preferred_element_type=jnp.float32)
    length = jnp.sum(head * head, axis=-1, keepdims=True)
    return (head * lax.rsqrt(length + 1e-06)).astype(jnp.bfloat16)


def pair_coef(fixed_rows, moving_rows, fixed_ids, moving_ids, scale, shift):
    logits = (
        scale
        * lax.dot_general(
            fixed_rows, moving_rows, (((1,), (1,)), ((), ())), preferred_element_type=jnp.float32
        )
        + shift
    )
    sign = jnp.where(fixed_ids[:, None] == moving_ids[None, :], jnp.float32(1.0), jnp.float32(-1.0))
    return (-sign * jax.nn.sigmoid(-sign * logits)).astype(jnp.bfloat16)


def pair_forces(fixed_rows, moving_rows, fixed_ids, moving_ids, scale, shift):
    coef = pair_coef(fixed_rows, moving_rows, fixed_ids, moving_ids, scale, shift)
    return jnp.dot(coef, moving_rows, preferred_element_type=jnp.float32)


def on_device(pooled, final_gain, head_weight, pair_ids, log_scale, bias):
    local_embed = embed_rows(pooled[0], final_gain[0], head_weight[0])
    count = local_embed.shape[0]
    scale = jnp.exp(log_scale[0])
    shift = bias[0]
    block_index = lax.axis_index("blk")
    local_ids = lax.dynamic_slice_in_dim(pair_ids, block_index * count, count)
    partner_embed = partner(local_embed, "tower", 0)
    total = pair_forces(
        local_embed,
        lax.all_gather(partner_embed, "blk", axis=0, tiled=True),
        local_ids,
        pair_ids,
        scale,
        shift,
    )
    return total[None]


def solution(mesh):
    placed = (P("tower", "blk", None), P("tower", None), P("tower", None, None), P(), P(), P())
    return jax.shard_map(
        on_device, mesh=mesh, in_specs=placed, out_specs=P("tower", "blk", None), check_vma=False
    )
```

profile of v0, /device:TPU:1, one launch (start us, length us, event | category | flops | bytes accessed | tf_op | source)
XLA Modules:
  0.0 296.5 jit_solution(8610071853615321268)
XLA Ops:
  6.5 0.0 copy-start
  6.5 0.0 all-gather.2.cloned.1.call-start
  6.5 1.2 convert_reduce_fusion
  7.8 1.2 fusion.23
  9.0 0.7 reduce.1
  9.7 0.0 copy-done
  9.7 1.7 multiply_reduce_fusion
  11.4 0.1 multiply_convert_fusion
  11.5 2.1 collective-permute-start
  13.7 5.5 %collective-permute-done = bf16[128,1152]{1,0:T(8,128)(2,1)S(1)} collective-permute-done((bf16[128,1152]{1,0:T(8,128)(2,1)S(1)}, bf16[128,1152]{1,0:T(8,128)(2,1)S(1)}, u32[]{:S(2)}, u32[]{:S(2)}) %collective-permute-start) | collective-permute-done | bytes 294944 | tf_op jit(solution)/shard_map/ppermute | solution.py:10
  19.1 0.0 copy-start.1
  19.1 0.7 copy-done.1
  19.8 0.0 all-gather.2.cloned.1.call-update
  21.2 0.8 dynamic_slice.3
  22.0 231.2 %all-gather.2.cloned.1.call-done = bf16[16384,1152]{1,0:T(8,128)(2,1)} async-done(((bf16[128,1152]{1,0:T(8,128)(2,1)}), bf16[16384,1152]{1,0:T(8,128)(2,1)}) %all-gather.2.cloned.1.call-update) | async-done | bytes 37748752 | tf_op jit(solution)/shard_map/all_gather | solution.py:50
  253.2 36.4 %fusion.17 = f32[1,128,1152]{2,1,0:T(8,128)} fusion(bf16[16384,1152]{1,0:T(8,128)(2,1)} %all-gather.2.cloned.1.call-done, bf16[128,1152]{1,0:T(8,128)(2,1)S(1)} %multiply_convert_fusion, f32[]{:T(128)} %bitcast.25, f32[]{:T(128)} %bitcast, s32[16384]{0:T(1024)} %param.9, s32[128]{0:T(128)S(1)} %dynamic_slice.3), kind=kOutput, calls=%fused_computation.18 | convolution fusion | flops 9686745088 | bytes 38699528 | tf_op jit(solution)/shard_map/dot_general | solution.py:37
  (3 shorter events, 0.0 us)
Async XLA Ops:
  6.5 3.2 %copy-start = (bf16[1,1152,1152]{2,1,0:T(8,128)(2,1)S(1)}, bf16[1,1152,1152]{2,1,0:T(8,128)(2,1)}, u32[]{:S(2)}) copy-start(bf16[1,1152,1152]{2,1,0:T(8,128)(2,1)} %param.8) | copy-start | bytes 7962628
  6.5 246.7 %all-gather.2.cloned.1.call-start = ((), (), s32[]{:S(2)}) async-start(), calls=%async_computation | async-start | bytes 38043648 | tf_op jit(solution)/shard_map/all_gather | solution.py:50
  11.5 7.6 %collective-permute-start = (bf16[128,1152]{1,0:T(8,128)(2,1)S(1)}, bf16[128,1152]{1,0:T(8,128)(2,1)S(1)}, u32[]{:S(2)}, u32[]{:S(2)}) collective-permute-start(bf16[128,1152]{1,0:T(8,128)(2,1)S(1)} %multiply_convert_fusion), channel_id=1, source_target_pairs={{0,128},{128,0},{1,129},{129,1},{2,130},{130,2},{3,131},{131,3},{4... | collective-permute-start | bytes 884744 | tf_op jit(solution)/shard_map/ppermute | solution.py:10
  19.1 0.7 copy-start.1
Sparse Core Ops, SparseCore 0:
  20.0 233.1 all-gather.1
where the time goes:
time: 297 us; the launch traced here: 296 us
  waiting for transfers between devices  237 us (80%)
  matrix products  38.1 us (13%)
  between operations  14.8 us (5%)
  other arithmetic  3.27 us (1%)
    all_gather x1, waiting for transfers between devices, on_device(): lax.all_gather(partner_embed, 'blk', axis=0, tiled=True)  231 us
    dot_general x1, matrix products, pair_forces(): return jnp.dot(coef, moving_rows, preferred_element_type=jnp.float32)  36.4 us
  transfers between devices with their start and end apart: 2, of which 2 were waited for; matrix products, arithmetic and copies ran while one was open for 0% of the time, Pallas kernels for 0%

commit v1 on v0

--- a/solution.py
+++ b/solution.py
@@ -47,7 +47,9 @@
     partner_embed = partner(local_embed, "tower", 0)
     total = pair_forces(
         local_embed,
-        lax.all_gather(partner_embed, "blk", axis=0, tiled=True),
+        jnp.concatenate(
+            lax.all_to_all(jnp.stack([partner_embed] * lax.axis_size("blk")), "blk", 0, 0), axis=0
+        ),
         local_ids,
         pair_ids,
         scale,

time: 297 us -> 939 us (3.16)
  waiting for transfers between devices: 237 us -> 856 us
  starting transfers between devices: 2.12 us -> 20.3 us
  between operations: 14.8 us -> 1.39 us
  local copies, waits for them, and re-layouts: 1.48 us -> 12.9 us
    all_to_all x0 -> x1, waiting for transfers between devices: none -> 850 us  [on_device(): lax.all_to_all(jnp.stack([partner_embed] * lax.axis_size('blk')), 'blk',...]
    all_gather x1 -> x0, waiting for transfers between devices: 231 us -> none  [on_device(): lax.all_gather(partner_embed, 'blk', axis=0, tiled=True)]
    all_to_all x0 -> x1, starting transfers between devices: none -> 18.2 us  [on_device(): lax.all_to_all(jnp.stack([partner_embed] * lax.axis_size('blk')), 'blk',...]
    another operation x0 -> x1, local copies, waits for them, and re-layouts: none -> 12.8 us  [on_device(): jnp.stack([partner_embed] * lax.axis_size('blk'))]
where the time goes in v1:
time: 939 us; the launch traced here: 932 us
  waiting for transfers between devices  856 us (91%)
  matrix products  38.1 us (4%)
  starting transfers between devices  20.3 us (2%)
  local copies, waits for them, and re-layouts  12.9 us (1%)
    all_to_all x1, waiting for transfers between devices, on_device(): lax.all_to_all(jnp.stack([partner_embed] * lax.axis_size('blk')), 'blk',...  850 us
    dot_general x1, matrix products, pair_forces(): return jnp.dot(coef, moving_rows, preferred_element_type=jnp.float32)  36.4 us
  transfers between devices with their start and end apart: 2, of which 2 were waited for; matrix products, arithmetic and copies ran while one was open for 0% of the time, Pallas kernels for 0%

profile of v1, /device:TPU:1, one launch (start us, length us, event | category | flops | bytes accessed | tf_op | source)
XLA Modules:
  0.0 931.8 jit_solution(15062305598932261297)
XLA Ops:
  0.0 0.0 copy-start
  0.0 1.2 convert_reduce_fusion
  1.2 1.2 fusion.23
  2.4 0.7 reduce.1
  3.2 0.0 copy-done
  3.2 1.7 multiply_reduce_fusion
  4.9 0.1 multiply_convert_fusion
  5.0 2.1 collective-permute-start
  7.1 5.5 collective-permute-done
  12.6 12.8 %stack.2 = bf16[128,128,1152]{2,1,0:T(8,128)(2,1)} broadcast(bf16[128,1152]{1,0:T(8,128)(2,1)S(1)} %collective-permute-done), dimensions={1,2} | broadcast | bytes 38043648 | tf_op jit(solution)/shard_map/stack | solution.py:51
  25.4 0.0 copy-start.2
  25.4 18.2 %all-to-all-start = ((bf16[128,128,1152]{2,1,0:T(8,128)(2,1)}), bf16[128,128,1152]{2,1,0:T(8,128)(2,1)}, u32[]{:S(2)}, u32[]{:S(2)}) async-start(bf16[128,128,1152]{2,1,0:T(8,128)(2,1)} %stack.2), calls=%async_computation | async-start | bytes 75497472 | tf_op jit(solution)/shard_map/all_to_all | solution.py:51
  44.9 0.0 copy-done.2
  44.9 0.1 dynamic_slice.3
  45.0 850.4 %all-to-all-done = bf16[128,128,1152]{2,1,0:T(8,128)(2,1)} async-done(((bf16[128,128,1152]{2,1,0:T(8,128)(2,1)}), bf16[128,128,1152]{2,1,0:T(8,128)(2,1)}, u32[]{:S(2)}, u32[]{:S(2)}) %all-to-all-start) | async-done | bytes 37748768 | tf_op jit(solution)/shard_map/all_to_all | solution.py:51
  895.4 0.0 copy-start.1
  895.4 36.4 %fusion.17 = f32[1,128,1152]{2,1,0:T(8,128)} fusion(bf16[16384,1152]{1,0:T(8,128)(2,1)} %bitcast.4, bf16[128,1152]{1,0:T(8,128)(2,1)S(1)} %multiply_convert_fusion, f32[]{:T(128)} %bitcast.26, f32[]{:T(128)} %bitcast, s32[16384]{0:T(1024)S(1)} %copy-done.2, s32[128]{0:T(128)S(1)} %dynamic_slice.3), kind=kOutput, calls=%fused_computation.18 | convolution fusion | flops 9686745088 | bytes 38699528 | tf_op jit(solution)/shard_map/dot_general | solution.py:37
  931.8 0.0 copy-done.1
  (3 shorter events, 0.0 us)
Async XLA Ops:
  0.0 3.2 copy-start
  5.0 7.6 collective-permute-start
  25.4 19.5 %copy-start.2 = (s32[16384]{0:T(1024)S(1)}, s32[16384]{0:T(1024)}, u32[]{:S(2)}) copy-start(s32[16384]{0:T(1024)} %param.9) | copy-start | bytes 196612
  25.4 870.0 %all-to-all-start = ((bf16[128,128,1152]{2,1,0:T(8,128)(2,1)}), bf16[128,128,1152]{2,1,0:T(8,128)(2,1)}, u32[]{:S(2)}, u32[]{:S(2)}) async-start(bf16[128,128,1152]{2,1,0:T(8,128)(2,1)} %stack.2), calls=%async_computation | async-start | bytes 75497472 | tf_op jit(solution)/shard_map/all_to_all | solution.py:51
  895.4 36.4 %copy-start.1 = (bf16[1,1152,1152]{2,1,0:T(8,128)(2,1)S(1)}, bf16[1,1152,1152]{2,1,0:T(8,128)(2,1)}, u32[]{:S(2)}) copy-start(bf16[1,1152,1152]{2,1,0:T(8,128)(2,1)} %param.8) | copy-start | bytes 7962628
